TPU v7x, 16 devices: a whole 2x2x2 slice. The times are simulated.
16 devices in a mesh: ep: 16 (over z, y, x, core).
Axes of the slice: x: 2, y: 2, z: 2, core: 2. Of those that a mesh axis runs over, the one named last changes fastest.
Arguments:
- x_in: bfloat16 [8192, 2560], P('ep')
- route_idx: int32 [8192, 6], P('ep')
- gate_w: bfloat16 [8192, 6], P('ep')
- dy_in: bfloat16 [8192, 2560], P('ep')
- w_gate: bfloat16 [16, 2560, 1536], P('ep')
- w_up: bfloat16 [16, 2560, 1536], P('ep')
- w_down: bfloat16 [16, 1536, 2560], P('ep')
- hot_gate: bfloat16 [2560, 1536], replicated
- hot_up: bfloat16 [2560, 1536], replicated
- hot_down: bfloat16 [1536, 2560], replicated
Outputs:
- output 1: bfloat16 [8192, 2560], P('ep')
- output 2: bfloat16 [8192, 2560], P('ep')
- output 3: float32 [16, 2560, 1536], P('ep')
- output 4: float32 [16, 2560, 1536], P('ep')
- output 5: float32 [16, 1536, 2560], P('ep')
- output 6: float32 [2560, 1536], P(None, 'ep')
- output 7: float32 [2560, 1536], P(None, 'ep')
- output 8: float32 [1536, 2560], P('ep')
All inputs are finite; a program needn't handle non-finite values.
Results may differ from a plain program's by a relative error of at most 0.00844653.
Values are sent between devices in bfloat16 or wider.
A program may use at most 1 GiB of HBM per device.

v0:
```python
import jax
import jax.numpy as jnp
from jax import lax
from jax.sharding import PartitionSpec as P


CONTRACT_LAST = (((1,), (1,)), ((), ()))
CONTRACT_FIRST = (((0,), (0,)), ((), ()))


def silu_parts(pre_gate):
    sig_val = jax.nn.sigmoid(pre_gate)
    return pre_gate * sig_val, sig_val * (1.0 + pre_gate * (1.0 - sig_val))


def dot_f32(lhs, rhs, dims=(((1,), (0,)), ((), ()))):
    return lax.dot_general(lhs, rhs, dims, preferred_element_type=jnp.float32)


def expert_forward(x_rows, gate_mat, up_mat, down_mat):
    u_val = dot_f32(x_rows, gate_mat)
    v_val = dot_f32(x_rows, up_mat)
    silu_val, silu_grad = silu_parts(u_val)
    hidden = (silu_val * v_val).astype(jnp.bfloat16)
    result = dot_f32(hidden, down_mat).astype(jnp.bfloat16)
    return result, hidden, v_val, silu_val, silu_grad


def hidden_grads(d_rows, v_val, silu_val, silu_grad, down_mat):
    grad_hidden = lax.reduce_precision(dot_f32(d_rows, down_mat, CONTRACT_LAST), 8, 7)
    grad_u = (grad_hidden * v_val * silu_grad).astype(jnp.bfloat16)
    grad_v = (grad_hidden * silu_val).astype(jnp.bfloat16)
    return grad_u, grad_v


def input_grad(grad_u, grad_v, gate_mat, up_mat):
    return (dot_f32(grad_u, gate_mat, CONTRACT_LAST) + dot_f32(grad_v, up_mat, CONTRACT_LAST)).astype(jnp.bfloat16)


def scaled(gate_col, rows):
    return (gate_col.astype(jnp.float32)[:, None] * rows.astype(jnp.float32)).astype(jnp.bfloat16)


def solution(mesh):
    n_dev = mesh.shape['ep']

    def local_body(x_loc, route_loc, gate_loc, dy_loc, w_gate, w_up, w_down, hot_gate, hot_up, hot_down):
        tok_rows, top_k = route_loc.shape
        d_model = x_loc.shape[1]
        d_ff = hot_gate.shape[1]
        part = d_ff // n_dev
        slot_cap = min(tok_rows, 2 * tok_rows * top_k // n_dev)
        w_gate, w_up, w_down = w_gate[0], w_up[0], w_down[0]
        me = lax.axis_index('ep')

        x_all = lax.all_gather(x_loc, 'ep', axis=0, tiled=True)
        dy_all = lax.all_gather(dy_loc, 'ep', axis=0, tiled=True)

        experts = jnp.arange(n_dev + 1, dtype=jnp.int32)
        picks = route_loc[:, :, None] == experts[None, None, :]
        gates = jnp.sum(jnp.where(picks, gate_loc.astype(jnp.float32)[:, :, None], 0.0), axis=1)
        member = jnp.any(picks, axis=1)
        token_ids = jnp.arange(tok_rows, dtype=jnp.int32)
        earlier = (token_ids[:, None] > token_ids[None, :]).astype(jnp.bfloat16)
        rank = dot_f32(earlier, member.astype(jnp.bfloat16))
        gate_hot = gates[:, n_dev]

        slot_rank = jnp.where(member, rank, -1.0)[:, :n_dev].T
        table = jnp.concatenate([slot_rank, gates[:, :n_dev].T, jnp.broadcast_to(gate_hot[None, :], (n_dev, tok_rows))], axis=1)
        table = lax.all_to_all(table, 'ep', 0, 0, tiled=True)
        rank_in = table[:, :tok_rows]
        gate_in = table[:, tok_rows:2 * tok_rows].astype(jnp.bfloat16)
        hot_in = table[:, 2 * tok_rows:3 * tok_rows].reshape(-1)

        out_hot, _, v_hot, silu_hot, sgrad_hot = expert_forward(x_loc, hot_gate, hot_up, hot_down)
        du_hot, dv_hot = hidden_grads(scaled(gate_hot, dy_loc), v_hot, silu_hot, sgrad_hot, hot_down)
        dx_hot = input_grad(du_hot, dv_hot, hot_gate, hot_up)

        cuts = (0, slot_cap // 3, slot_cap)
        chunks = tuple(zip(cuts[:-1], cuts[1:]))
        regular = picks[:, :, :n_dev]
        mixes = []
        for low, high in chunks:
            inside = (rank[:, :n_dev] >= low) & (rank[:, :n_dev] < high)
            place = jnp.arange(n_dev, dtype=jnp.float32)[None, :] * (high - low) + (rank[:, :n_dev] - low)
            dest = jnp.sum(jnp.where(regular & inside[:, None, :], place[:, None, :] + 1.0, 0.0), axis=2) - 1.0
            hits = dest[:, :, None] == jnp.arange(n_dev * (high - low), dtype=jnp.float32)[None, None, :]
            gate_mix = jnp.sum(jnp.where(hits, gate_loc.astype(jnp.float32)[:, :, None], 0.0), axis=1).astype(jnp.bfloat16)
            mixes.append((gate_mix, jnp.any(hits, axis=1).astype(jnp.bfloat16)))

        x_all, out_hot, dx_hot, mixes = lax.optimization_barrier((x_all, out_hot, dx_hot, mixes))
        batched = (((2,), (1,)), ((0,), (0,)))

        def match_of(low, high):
            return rank_in[:, None, :] == jnp.arange(low, high, dtype=jnp.float32)[None, :, None]

        def pick(weights, rows):
            got = dot_f32(weights, rows.reshape(n_dev, tok_rows, d_model), batched)
            return got.astype(jnp.bfloat16).reshape(-1, d_model)

        def send_back(rows):
            return lax.all_to_all(rows, 'ep', 0, 0, tiled=True)

        def forward(bounds, x_all):
            x_rows = pick(match_of(*bounds).astype(jnp.bfloat16), x_all)
            return x_rows, expert_forward(x_rows, w_gate, w_up, w_down)

        def backward(bounds, dy_all, saved):
            q_rows = pick(jnp.where(match_of(*bounds), gate_in[:, None, :], jnp.bfloat16(0)), dy_all)
            du_val, dv_val = hidden_grads(q_rows, *saved, w_down)
            return q_rows, du_val, dv_val, input_grad(du_val, dv_val, w_gate, w_up)

        x_a, (out_a, hidden_a, *saved_a) = forward(chunks[0], x_all)
        out_a, x_all = lax.optimization_barrier((out_a, x_all))
        out_back_a = send_back(out_a)
        x_b, (out_b, hidden_b, *saved_b) = forward(chunks[1], x_all)
        order = lax.optimization_barrier
        out_back_a, out_b, dy_all, x_all = order((out_back_a, out_b, dy_all, x_all))
        out_back_b = send_back(out_b)
        q_b, du_b, dv_b, dx_b = backward(chunks[1], dy_all, saved_b)
        dx_b, x_all, dy_all = order((dx_b, x_all, dy_all))

        first_unit = me * part
        hg = lax.dynamic_slice_in_dim(hot_gate, first_unit, part, 1)
        hu = lax.dynamic_slice_in_dim(hot_up, first_unit, part, 1)
        hd = lax.dynamic_slice_in_dim(hot_down, first_unit, part, 0)
        uv = dot_f32(x_all, jnp.concatenate([hg, hu], axis=1))
        silu_p, sgrad_p = silu_parts(uv[:, :part])
        v_p = uv[:, part:]
        hid_p = (silu_p * v_p).astype(jnp.bfloat16)
        q_all = scaled(hot_in, dy_all)
        du_p, dv_p = hidden_grads(q_all, v_p, silu_p, sgrad_p, hd)
        dguh = dot_f32(x_all, jnp.concatenate([du_p, dv_p], axis=1), CONTRACT_FIRST)
        hot_ddown = dot_f32(hid_p, q_all, CONTRACT_FIRST)

        out_back_b, dx_b, dguh, hot_ddown, dy_all = order((out_back_b, dx_b, dguh, hot_ddown, dy_all))
        dx_back_b = send_back(dx_b)

        def both(rows_a, grads_a, rows_b, grads_b):
            return dot_f32(rows_b, grads_b, CONTRACT_FIRST) + dot_f32(rows_a, grads_a, CONTRACT_FIRST)

        q_a, du_a, dv_a, dx_a = backward(chunks[0], dy_all, saved_a)
        grad_down = both(hidden_a, q_a, hidden_b, q_b)
        grad_up = both(x_a, dv_a, x_b, dv_b)
        dx_back_b, dx_a, grad_down, grad_up, du_a, du_b, out_back_a, out_back_b = order(
            (dx_back_b, dx_a, grad_down, grad_up, du_a, du_b, out_back_a, out_back_b))
        dx_back_a = send_back(dx_a)
        grad_gate = both(x_a, du_a, x_b, du_b)

        (gate_mix_a, plain_mix_a), (gate_mix_b, plain_mix_b) = mixes
        y_loc = dot_f32(gate_mix_b, out_back_b) + dot_f32(gate_mix_a, out_back_a) + gate_hot[:, None] * out_hot.astype(jnp.float32)
        dx_part = dot_f32(plain_mix_b, dx_back_b) + dx_hot.astype(jnp.float32)
        dx_part = lax.optimization_barrier(dx_part)
        dx_loc = dot_f32(plain_mix_a, dx_back_a) + dx_part
        return (y_loc.astype(jnp.bfloat16), dx_loc.astype(jnp.bfloat16), grad_gate[None], grad_up[None], grad_down[None],
                dguh[:, :part], dguh[:, part:], hot_ddown)

    row_spec = P('ep', None)
    expert_spec = P('ep', None, None)
    whole_spec = P(None, None)
    return jax.shard_map(local_body, mesh=mesh, in_specs=(row_spec, row_spec, row_spec, row_spec, expert_spec, expert_spec, expert_spec, whole_spec, whole_spec, whole_spec), out_specs=(row_spec, row_spec, expert_spec, expert_spec, expert_spec, P(None, 'ep'), P(None, 'ep'), P('ep', None)), check_vma=False)
```

profile of v0, /device:TPU:0, one launch (start us, length us, event | category | flops | bytes accessed | tf_op | source)
XLA Modules:
  0.0 1165.3 jit_solution(17880592700459732580)
XLA Ops:
  12.0 5.3 all-to-all-start
  22.7 13.0 %fusion = pred[512,4096]{1,0:T(8,128)(4,1)S(1)} fusion(f32[512,6]{0,1:T(8,128)S(1)} %broadcast_add_fusion), kind=kLoop, calls=%fused_computation.3 | loop fusion | flops 23068672 | bytes 2109440 | tf_op jit(solution)/shard_map/reduce_or | solution.py:89
  45.5 11.8 %fusion.69 = f32[512,1536]{1,0:T(8,128)} fusion(bf16[512,2560]{1,0:T(8,128)(2,1)} %param.10, bf16[2560,1536]{1,0:T(8,128)(2,1)} %param.17), kind=kOutput, calls=%fused_computation.128 | convolution fusion | flops 4026531840 | bytes 13631488 | tf_op jit(solution)/shard_map/dot_general | solution.py:17
  57.3 5.9 fusion.70
  63.3 6.0 convolution_reduce-precision_fusion
  69.3 6.7 convolution_convert_fusion.6
  76.0 13.1 %select_reduce_fusion = bf16[512,4096]{1,0:T(8,128)(2,1)} fusion(f32[512,6]{0,1:T(8,128)S(1)} %convert_element_type.114, f32[512,6]{0,1:T(8,128)S(1)} %broadcast_add_fusion), kind=kLoop, calls=%fused_computation.1 | loop fusion | flops 35651584 | bytes 4218880 | tf_op jit(solution)/shard_map/reduce_sum | solution.py:88
  89.1 14.3 %fusion.45 = f32[512,2560]{1,0:T(8,128)S(1)} fusion(bf16[2560,1536]{1,0:T(8,128)(2,1)} %param.17, f32[512,1536]{1,0:T(8,128)} %fusion.69, f32[512,1536]{1,0:T(8,128)} %convolution_reduce-precision_fusion, f32[512,1536]{1,0:T(8,128)} %fusion.70), kind=kOutput, calls=%fused_computation.85 | convolution fusion | flops 4034396160 | bytes 22544384 | tf_op jit(solution)/shard_map/dot_general | solution.py:17
  103.4 10.1 add_convert_fusion.4
  115.3 56.5 %all-gather.3.cloned.1.call-done = bf16[8192,2560]{1,0:T(8,128)(2,1)} async-done(((bf16[512,2560]{1,0:T(8,128)(2,1)}), bf16[8192,2560]{1,0:T(8,128)(2,1)}) %all-gather.3.cloned.1.call-update) | async-done | bytes 41943056 | tf_op jit(solution)/shard_map/all_gather | solution.py:56
  171.8 28.7 %convolution_convert_fusion.5 = bf16[16,128,2560]{2,1,0:T(8,128)(2,1)} fusion(bf16[16,512,2560]{2,1,0:T(8,128)(2,1)} %bitcast.117, f32[16,512]{1,0:T(8,128)S(1)} %get-tuple-element.77), kind=kOutput, calls=%fused_computation.32 | convolution fusion | flops 5375000576 | bytes 52461568 | tf_op jit(solution)/shard_map/dot_general | solution.py:17
  200.5 23.1 %fusion.26 = f32[2048,1536]{1,0:T(8,128)} fusion(bf16[2048,2560]{1,0:T(8,128)(2,1)} %bitcast.127, bf16[1,2560,1536]{2,1,0:T(8,128)(2,1)} %param.14), kind=kOutput, calls=%fused_computation.51 | convolution fusion | flops 16106127360 | bytes 30932992 | tf_op jit(solution)/shard_map/dot_general | solution.py:17
  223.7 25.0 %multiply_convert_fusion.8 = (bf16[2048,1536]{1,0:T(8,128)(2,1)}, f32[2048,1536]{1,0:T(8,128)}) fusion(f32[2048,1536]{1,0:T(8,128)} %fusion.26, bf16[2048,2560]{1,0:T(8,128)(2,1)S(1)} %bitcast.130, bf16[1,2560,1536]{2,1,0:T(8,128)(2,1)} %param.15), kind=kOutput, calls=%fused_computation.24 | convolution fusion | flops 16125001728 | bytes 49807360 | tf_op jit(solution)/shard_map/dot_general | solution.py:17
  248.7 23.6 %convolution_convert_fusion.3 = bf16[2048,2560]{1,0:T(8,128)(2,1)} fusion(bf16[2048,1536]{1,0:T(8,128)(2,1)} %get-tuple-element.85, bf16[1,1536,2560]{2,1,0:T(8,128)(2,1)} %param.16), kind=kOutput, calls=%fused_computation.27 | convolution fusion | flops 16111370240 | bytes 24641536 | tf_op jit(solution)/shard_map/dot_general | solution.py:17
  272.3 4.1 all-to-all-start.1
  276.4 22.9 %convolution_convert_fusion.2 = bf16[16,256,2560]{2,1,0:T(8,128)(2,1)} fusion(bf16[16,512,2560]{2,1,0:T(8,128)(2,1)} %bitcast.118, f32[16,512]{1,0:T(8,128)S(1)} %get-tuple-element.77, f32[256]{0:T(256)S(1)} %copy-done.15), kind=kOutput, calls=%fused_computation.16 | convolution fusion | flops 10750001152 | bytes 62948352 | tf_op jit(solution)/shard_map/dot_general | solution.py:17
  299.3 40.7 %fusion.24 = f32[4096,1536]{1,0:T(8,128)} fusion(bf16[4096,2560]{1,0:T(8,128)(2,1)} %bitcast.121, bf16[1,2560,1536]{2,1,0:T(8,128)(2,1)} %param.14), kind=kOutput, calls=%fused_computation.49 | convolution fusion | flops 32212254720 | bytes 54001664 | tf_op jit(solution)/shard_map/dot_general | solution.py:17
  340.0 43.7 %multiply_convert_fusion.3 = (bf16[4096,1536]{1,0:T(8,128)(2,1)}, f32[4096,1536]{1,0:T(8,128)}) fusion(f32[4096,1536]{1,0:T(8,128)} %fusion.24, bf16[4096,2560]{1,0:T(8,128)(2,1)} %bitcast.122, bf16[1,2560,1536]{2,1,0:T(8,128)(2,1)} %param.15), kind=kOutput, calls=%fused_computation.7 | convolution fusion | flops 32250003456 | bytes 91750400 | tf_op jit(solution)/shard_map/dot_general | solution.py:17
  383.7 37.4 %convolution_convert_fusion = bf16[4096,2560]{1,0:T(8,128)(2,1)} fusion(bf16[4096,1536]{1,0:T(8,128)(2,1)} %get-tuple-element.87, bf16[1,1536,2560]{2,1,0:T(8,128)(2,1)S(1)} %bitcast.147), kind=kOutput, calls=%fused_computation.13 | convolution fusion | flops 32222740480 | bytes 41418752 | tf_op jit(solution)/shard_map/dot_general | solution.py:17
  421.2 10.0 all-gather.5.cloned.1.call-done
  431.2 16.9 %all-to-all-done.1 = bf16[16,128,2560]{2,1,0:T(8,128)(2,1)} async-done(((bf16[16,128,2560]{2,1,0:T(8,128)(2,1)}), bf16[16,128,2560]{2,1,0:T(8,128)(2,1)}, u32[]{:S(2)}, u32[]{:S(2)}) %all-to-all-start.1) | async-done | bytes 10485792 | tf_op jit(solution)/shard_map/all_to_all | solution.py:102
  448.1 4.2 all-to-all-start.2
  452.3 22.9 %convolution_convert_fusion.1 = bf16[16,256,2560]{2,1,0:T(8,128)(2,1)} fusion(bf16[16,512,2560]{2,1,0:T(8,128)(2,1)} %bitcast.115, f32[16,512]{1,0:T(8,128)S(1)} %copy-done.2, f32[256]{0:T(256)S(1)} %copy-done.16, bf16[16,512]{1,0:T(8,128)(2,1)S(1)} %copy-done.10), kind=kOutput, calls=%fused_computation.15 | convolution fusion | flops 10752098304 | bytes 62964736 | tf_op jit(solution)/shard_map/dot_general | solution.py:17
  475.2 48.2 %multiply_convert_fusion.1 = (bf16[4096,1536]{1,0:T(8,128)(2,1)}, bf16[4096,1536]{1,0:T(8,128)(2,1)}) fusion(f32[4096,1536]{1,0:T(8,128)} %fusion.24, f32[4096,1536]{1,0:T(8,128)} %get-tuple-element.88, bf16[4096,2560]{1,0:T(8,128)(2,1)} %bitcast.119, bf16[1,1536,2560]{2,1,0:T(8,128)(2,1)} %param.16), kind=kOutput, calls=%fused_computation.5 | convolution fusion | flops 32300335104 | bytes 104333312 | tf_op jit(solution)/shard_map/dot_general | solution.py:17
  523.4 41.4 %fusion.22 = f32[4096,2560]{1,0:T(8,128)} fusion(bf16[4096,1536]{1,0:T(8,128)(2,1)} %get-tuple-element.60, bf16[1,2560,1536]{2,1,0:T(8,128)(2,1)} %param.14), kind=kOutput, calls=%fused_computation.47 | convolution fusion | flops 32212254720 | bytes 62390272 | tf_op jit(solution)/shard_map/dot_general | solution.py:17
  564.8 43.9 %add_convert_fusion = bf16[4096,2560]{1,0:T(8,128)(2,1)} fusion(f32[4096,2560]{1,0:T(8,128)} %fusion.22, bf16[4096,1536]{1,0:T(8,128)(2,1)} %get-tuple-element.68, bf16[1,2560,1536]{2,1,0:T(8,128)(2,1)} %param.15), kind=kOutput, calls=%fused_computation.4 | convolution fusion | flops 32233226240 | bytes 83361792 | tf_op jit(solution)/shard_map/dot_general | solution.py:17
  608.7 22.2 %fusion.47 = f32[8192,192]{0,1:T(8,128)} fusion(bf16[8192,2560]{1,0:T(8,128)(2,1)} %all-gather.3.cloned.1.call-done, bf16[2560,96]{1,0:T(8,128)(2,1)S(1)} %copy-done.13, bf16[2560,96]{1,0:T(8,128)(2,1)S(1)} %copy-done.14), kind=kOutput, calls=%fused_computation.87 | convolution fusion | flops 8055029760 | bytes 49217536 | tf_op jit(solution)/shard_map/dot_general | solution.py:17
  630.9 22.4 %multiply_convert_fusion.14 = (bf16[8192,96]{0,1:T(8,128)(2,1)S(1)}, bf16[8192,96]{0,1:T(8,128)(2,1)}) fusion(f32[8192,192]{0,1:T(8,128)} %fusion.47, bf16[1536,2560]{1,0:T(8,128)(2,1)} %param.19, s32[]{:T(128)S(6)} %select_n.43, bf16[8192,2560]{1,0:T(8,128)(2,1)} %all-gather.5.cloned.1.call-done, f32[8192]{0:T(1024)S(1)} %bitcast.139), kind=kOutput, calls=%fused_computation.72 | convolution fusion | flops 4100456448 | bytes 51904516 | tf_op jit(solution)/shard_map/dot_general | solution.py:17
  653.3 18.9 %fusion.33 = f32[2560,192]{0,1:T(8,128)} fusion(bf16[8192,2560]{1,0:T(8,128)(2,1)} %all-gather.3.cloned.1.call-done, bf16[8192,96]{0,1:T(8,128)(2,1)} %get-tuple-element.73, bf16[8192,96]{0,1:T(8,128)(2,1)S(1)} %get-tuple-element.72), kind=kOutput, calls=%fused_computation.66 | convolution fusion | flops 8059355136 | bytes 47054848 | tf_op jit(solution)/shard_map/dot_general | solution.py:17
  672.3 19.6 %fusion.3 = f32[96,2560]{1,0:T(8,128)} fusion(bf16[8192,2560]{1,0:T(8,128)(2,1)} %all-gather.5.cloned.1.call-done, f32[8192]{0:T(1024)S(1)} %bitcast.140, f32[8192,192]{0,1:T(8,128)} %fusion.47), kind=kOutput, calls=%fused_computation.17 | convolution fusion | flops 4094164992 | bytes 49250304 | tf_op jit(solution)/shard_map/dot_general | solution.py:17
  691.9 41.5 %fusion.71 = f32[1536,2560]{1,0:T(8,128)} fusion(bf16[4096,1536]{1,0:T(8,128)(2,1)} %get-tuple-element.87, bf16[4096,2560]{1,0:T(8,128)(2,1)} %bitcast.120), kind=kOutput, calls=%fused_computation.130 | convolution fusion | flops 32212254720 | bytes 49283072 | tf_op jit(solution)/shard_map/dot_general | solution.py:17
  733.4 28.7 %convolution_convert_fusion.4 = bf16[16,128,2560]{2,1,0:T(8,128)(2,1)} fusion(bf16[16,512,2560]{2,1,0:T(8,128)(2,1)} %bitcast.116, f32[16,512]{1,0:T(8,128)S(1)} %copy-done.3, bf16[16,512]{1,0:T(8,128)(2,1)S(1)} %copy-done.11), kind=kOutput, calls=%fused_computation.31 | convolution fusion | flops 5376049152 | bytes 52477952 | tf_op jit(solution)/shard_map/dot_general | solution.py:17
  762.1 4.5 all-to-all-start.3
  766.6 32.4 %multiply_convert_fusion.6 = (bf16[2048,1536]{1,0:T(8,128)(2,1)}, bf16[2048,1536]{1,0:T(8,128)(2,1)}) fusion(f32[2048,1536]{1,0:T(8,128)} %fusion.26, f32[2048,1536]{1,0:T(8,128)} %get-tuple-element.86, bf16[2048,2560]{1,0:T(8,128)(2,1)} %bitcast.131, bf16[1,1536,2560]{2,1,0:T(8,128)(2,1)} %param.16), kind=kOutput, calls=%fused_computation.22 | convolution fusion | flops 16150167552 | bytes 56098816 | tf_op jit(solution)/shard_map/dot_general | solution.py:17
  799.0 23.1 %fusion.20 = f32[2048,2560]{1,0:T(8,128)} fusion(bf16[2048,1536]{1,0:T(8,128)(2,1)} %get-tuple-element.61, bf16[1,2560,1536]{2,1,0:T(8,128)(2,1)} %param.14), kind=kOutput, calls=%fused_computation.45 | convolution fusion | flops 16106127360 | bytes 35127296 | tf_op jit(solution)/shard_map/dot_general | solution.py:17
  822.1 25.0 %add_convert_fusion.1 = bf16[2048,2560]{1,0:T(8,128)(2,1)} fusion(f32[2048,2560]{1,0:T(8,128)} %fusion.20, bf16[2048,1536]{1,0:T(8,128)(2,1)} %get-tuple-element.70, bf16[1,2560,1536]{2,1,0:T(8,128)(2,1)} %param.15), kind=kOutput, calls=%fused_computation.14 | convolution fusion | flops 16116613120 | bytes 45613056 | tf_op jit(solution)/shard_map/dot_general | solution.py:17
  848.5 21.5 %fusion.72 = f32[2560,1536]{1,0:T(8,128)S(1)} fusion(bf16[2048,2560]{1,0:T(8,128)(2,1)} %bitcast.128, bf16[2048,1536]{1,0:T(8,128)(2,1)} %get-tuple-element.70), kind=kOutput, calls=%fused_computation.131 | convolution fusion | flops 16106127360 | bytes 32505856 | tf_op jit(solution)/shard_map/dot_general | solution.py:17
  870.0 25.7 %convolution_add_fusion.1 = f32[1536,2560]{1,0:T(8,128)} fusion(f32[1536,2560]{1,0:T(8,128)} %fusion.71, bf16[2048,1536]{1,0:T(8,128)(2,1)} %get-tuple-element.85, bf16[2048,2560]{1,0:T(8,128)(2,1)} %bitcast.132), kind=kOutput, calls=%fused_computation.21 | convolution fusion | flops 16110059520 | bytes 48234496 | tf_op jit(solution)/shard_map/dot_general | solution.py:17
  895.7 42.1 %convolution_add_fusion = f32[2560,1536]{1,0:T(8,128)} fusion(f32[2560,1536]{1,0:T(8,128)S(1)} %fusion.72, bf16[4096,2560]{1,0:T(8,128)(2,1)} %bitcast.123, bf16[4096,1536]{1,0:T(8,128)(2,1)} %get-tuple-element.68), kind=kOutput, calls=%fused_computation.20 | convolution fusion | flops 32216186880 | bytes 65011712 | tf_op jit(solution)/shard_map/dot_general | solution.py:17
  937.7 77.6 %all-to-all-done.3 = bf16[16,256,2560]{2,1,0:T(8,128)(2,1)} async-done(((bf16[16,256,2560]{2,1,0:T(8,128)(2,1)}), bf16[16,256,2560]{2,1,0:T(8,128)(2,1)}, u32[]{:S(2)}, u32[]{:S(2)}) %all-to-all-start.3) | async-done | bytes 20971552 | tf_op jit(solution)/shard_map/all_to_all | solution.py:102
  1015.4 5.0 all-to-all-start.4
  1020.4 22.8 %fusion.74 = f32[2560,1536]{1,0:T(8,128)} fusion(bf16[2048,2560]{1,0:T(8,128)(2,1)} %bitcast.129, bf16[2048,1536]{1,0:T(8,128)(2,1)} %get-tuple-element.61), kind=kOutput, calls=%fused_computation.133 | convolution fusion | flops 16106127360 | bytes 32505856 | tf_op jit(solution)/shard_map/dot_general | solution.py:17
  1043.3 16.9 %convert_add_fusion = f32[512,2560]{1,0:T(8,128)} fusion(bf16[512,2560]{1,0:T(8,128)(2,1)S(1)} %copy-done.23, bf16[512,4096]{1,0:T(8,128)(2,1)S(1)} %copy-done.4, bf16[4096,2560]{1,0:T(8,128)(2,1)} %bitcast.18), kind=kOutput, calls=%fused_computation.54 | convolution fusion | flops 10740039680 | bytes 33030144 | tf_op jit(solution)/shard_map/dot_general | solution.py:17
  1060.2 8.4 fusion.73
  1068.7 16.5 %add_convert_fusion.3 = bf16[512,2560]{1,0:T(8,128)(2,1)} fusion(bf16[512,2560]{1,0:T(8,128)(2,1)S(1)} %copy-done.24, f32[512,2560]{1,0:T(8,128)S(1)} %fusion.73, bf16[512,4096]{1,0:T(8,128)(2,1)S(1)} %copy-done.5, bf16[4096,2560]{1,0:T(8,128)(2,1)} %bitcast.14, f32[512]{0:T(512)S(1)} %bitcast.143), kind=kOutput, calls=%fused_computation.55 | convolution fusion | flops 10743971840 | bytes 35653632 | tf_op jit(solution)/shard_map/dot_general | solution.py:17
  1085.2 42.3 %add_bitcast_fusion = f32[1,2560,1536]{2,1,0:T(8,128)} fusion(f32[2560,1536]{1,0:T(8,128)} %fusion.74, bf16[4096,2560]{1,0:T(8,128)(2,1)} %bitcast.124, bf16[4096,1536]{1,0:T(8,128)(2,1)} %get-tuple-element.60), kind=kOutput, calls=%fused_computation.19 | convolution fusion | flops 32216186880 | bytes 65011712 | tf_op jit(solution)/shard_map/dot_general | solution.py:17
  1127.5 19.2 %all-to-all-done.4 = bf16[16,128,2560]{2,1,0:T(8,128)(2,1)} async-done(((bf16[16,128,2560]{2,1,0:T(8,128)(2,1)}), bf16[16,128,2560]{2,1,0:T(8,128)(2,1)}, u32[]{:S(2)}, u32[]{:S(2)}) %all-to-all-start.4) | async-done | bytes 10485792 | tf_op jit(solution)/shard_map/all_to_all | solution.py:102
  1146.7 11.6 add_convert_fusion.2
  (97 shorter events, 23.3 us)
Async XLA Ops:
  7.2 164.7 %all-gather.3.cloned.1.call-start = ((), (), s32[]{:S(2)}) async-start(), calls=%async_computation.5 | async-start | bytes 44564480 | tf_op jit(solution)/shard_map/all_gather | solution.py:56
  7.9 423.3 %all-gather.5.cloned.1.call-start = ((), (), s32[]{:S(2)}) async-start(), calls=%async_computation.6 | async-start | bytes 44564480 | tf_op jit(solution)/shard_map/all_gather | solution.py:57
  10.1 53.1 %copy-start.18 = (f32[512,1]{0,1:T(1,128)}, f32[512,1]{0,1:T(1,128)S(1)}, u32[]{:S(2)}) copy-start(f32[512,1]{0,1:T(1,128)S(1)} %slice.54) | copy-start | bytes 6148
  12.0 102.1 %all-to-all-start = ((f32[16,1,1536]{2,1,0:T(1,128)}), f32[16,1,1536]{2,1,0:T(1,128)S(1)}, u32[]{:S(2)}, u32[]{:S(2)}) async-start(f32[16,1,1536]{2,1,0:T(1,128)} %copy.37), calls=%async_computation | async-start | bytes 196608 | tf_op jit(solution)/shard_map/all_to_all | solution.py:70
  41.7 15.6 %slice-start = ((s8[7864320]{0:T(1024)(128)(4,1)}), s8[3670016]{0:T(1024)(128)(4,1)S(1)}, s32[]{:S(2)}) async-start(s8[7864320]{0:T(1024)(128)(4,1)} %bitcast.137), calls=%async_computation.7 | async-start | bytes 7340032
  45.5 11.8 %copy-start.6 = (bf16[512,2560]{1,0:T(8,128)(2,1)S(1)}, bf16[512,2560]{1,0:T(8,128)(2,1)}, u32[]{:S(2)}) copy-start(bf16[512,2560]{1,0:T(8,128)(2,1)} %param.10) | copy-start | bytes 7864324
  45.5 11.8 %slice-start.1 = ((s8[7864320]{0:T(1024)(128)(4,1)}), s8[4194304]{0:T(1024)(128)(4,1)S(1)}, s32[]{:S(2)}) async-start(s8[7864320]{0:T(1024)(128)(4,1)} %bitcast.137), calls=%async_computation.8 | async-start | bytes 8388608
  45.5 17.7 %slice-start.2 = ((s8[7864320]{0:T(1024)(128)(4,1)}), s8[4194304]{0:T(1024)(128)(4,1)S(1)}, s32[]{:S(2)}) async-start(s8[7864320]{0:T(1024)(128)(4,1)} %bitcast.144), calls=%async_computation.9 | async-start | bytes 8388608
  57.3 5.9 copy-start.7
  57.3 5.9 slice-start.3
  63.3 6.0 copy-start.20
  63.3 6.0 copy-start.22
  89.1 14.3 %copy-start.21 = (f32[512,1536]{1,0:T(8,128)S(1)}, f32[512,1536]{1,0:T(8,128)}, u32[]{:S(2)}) copy-start(f32[512,1536]{1,0:T(8,128)} %fusion.69) | copy-start | bytes 9437188
  114.7 161.7 %copy-start.1 = (f32[16,512]{1,0:T(8,128)}, f32[16,512]{1,0:T(8,128)S(1)}, u32[]{:S(2)}) copy-start(f32[16,512]{1,0:T(8,128)S(1)} %get-tuple-element.77) | copy-start | bytes 98308
  200.5 23.1 %copy-start = (bf16[16,128,2560]{2,1,0:T(8,128)(2,1)S(1)}, bf16[16,128,2560]{2,1,0:T(8,128)(2,1)}, u32[]{:S(2)}) copy-start(bf16[16,128,2560]{2,1,0:T(8,128)(2,1)} %convolution_convert_fusion.5) | copy-start | bytes 31457284
  272.3 4.1 copy-start.15
  272.3 175.8 %all-to-all-start.1 = ((bf16[16,128,2560]{2,1,0:T(8,128)(2,1)}), bf16[16,128,2560]{2,1,0:T(8,128)(2,1)}, u32[]{:S(2)}, u32[]{:S(2)}) async-start(bf16[16,128,2560]{2,1,0:T(8,128)(2,1)} %bitcast.134), calls=%async_computation.1 | async-start | bytes 20971520 | tf_op jit(solution)/shard_map/all_to_all | solution.py:102
  299.3 84.4 %slice-start.4 = ((s8[7864320]{0:T(1024)(128)(4,1)}), s8[4194304]{0:T(1024)(128)(4,1)S(1)}, s32[]{:S(2)}) async-start(s8[7864320]{0:T(1024)(128)(4,1)} %bitcast.146), calls=%async_computation.11 | async-start | bytes 8388608
  340.0 43.8 %slice-start.5 = ((s8[7864320]{0:T(1024)(128)(4,1)}), s8[3670016]{0:T(1024)(128)(4,1)S(1)}, s32[]{:S(2)}) async-start(s8[7864320]{0:T(1024)(128)(4,1)} %bitcast.146), calls=%async_computation.12 | async-start | bytes 7340032
  448.0 4.2 copy-start.2
  448.0 4.2 copy-start.10
  448.0 4.3 copy-start.16
  448.1 285.4 %all-to-all-start.2 = ((bf16[16,256,2560]{2,1,0:T(8,128)(2,1)}), bf16[16,256,2560]{2,1,0:T(8,128)(2,1)}, u32[]{:S(2)}, u32[]{:S(2)}) async-start(bf16[16,256,2560]{2,1,0:T(8,128)(2,1)} %bitcast.126), calls=%async_computation.2 | async-start | bytes 41943040 | tf_op jit(solution)/shard_map/all_to_all | solution.py:102
  564.8 43.9 %copy-start.13 = (bf16[2560,96]{1,0:T(8,128)(2,1)S(1)}, bf16[2560,96]{1,0:T(8,128)(2,1)}, u32[]{:S(2)}) copy-start(bf16[2560,96]{1,0:T(8,128)(2,1)} %get-tuple-element.91) | copy-start | bytes 1474564
  564.8 43.9 %copy-start.14 = (bf16[2560,96]{1,0:T(8,128)(2,1)S(1)}, bf16[2560,96]{1,0:T(8,128)(2,1)}, u32[]{:S(2)}) copy-start(bf16[2560,96]{1,0:T(8,128)(2,1)} %get-tuple-element.92) | copy-start | bytes 1474564
  608.7 22.2 %copy-start.17 = (f32[2,4,8,128]{3,1,2,0:T(4,128)S(1)}, f32[2,4,8,128]{3,1,2,0:T(4,128)}, u32[]{:S(2)}) copy-start(f32[2,4,8,128]{3,1,2,0:T(4,128)} %copy.43) | copy-start | bytes 98308
  691.9 41.5 %copy-start.3 = (f32[16,512]{1,0:T(8,128)S(1)}, f32[16,512]{1,0:T(8,128)}, u32[]{:S(2)}) copy-start(f32[16,512]{1,0:T(8,128)} %copy-done.1) | copy-start | bytes 98308
  691.9 41.5 %copy-start.11 = (bf16[16,512]{1,0:T(8,128)(2,1)S(1)}, bf16[16,512]{1,0:T(8,128)(2,1)}, u32[]{:S(2)}) copy-start(bf16[16,512]{1,0:T(8,128)(2,1)} %slice.86) | copy-start | bytes 49156
  762.1 253.3 %all-to-all-start.3 = ((bf16[16,256,2560]{2,1,0:T(8,128)(2,1)}), bf16[16,256,2560]{2,1,0:T(8,128)(2,1)}, u32[]{:S(2)}, u32[]{:S(2)}) async-start(bf16[16,256,2560]{2,1,0:T(8,128)(2,1)} %bitcast.125), calls=%async_computation.3 | async-start | bytes 41943040 | tf_op jit(solution)/shard_map/all_to_all | solution.py:102
  822.1 25.0 %copy-start.12 = (f32[2560,192]{0,1:T(8,128)S(1)}, f32[2560,192]{0,1:T(8,128)}, u32[]{:S(2)}) copy-start(f32[2560,192]{0,1:T(8,128)} %fusion.33) | copy-start | bytes 5898244
  1015.4 131.3 %all-to-all-start.4 = ((bf16[16,128,2560]{2,1,0:T(8,128)(2,1)}), bf16[16,128,2560]{2,1,0:T(8,128)(2,1)}, u32[]{:S(2)}, u32[]{:S(2)}) async-start(bf16[16,128,2560]{2,1,0:T(8,128)(2,1)} %bitcast.133), calls=%async_computation.4 | async-start | bytes 20971520 | tf_op jit(solution)/shard_map/all_to_all | solution.py:102
  1020.4 22.9 %copy-start.4 = (bf16[512,4096]{1,0:T(8,128)(2,1)S(1)}, bf16[512,4096]{1,0:T(8,128)(2,1)}, u32[]{:S(2)}) copy-start(bf16[512,4096]{1,0:T(8,128)(2,1)} %convert_element_type.123) | copy-start | bytes 12582916
  1020.4 22.9 %copy-start.23 = (bf16[512,2560]{1,0:T(8,128)(2,1)S(1)}, bf16[512,2560]{1,0:T(8,128)(2,1)}, u32[]{:S(2)}) copy-start(bf16[512,2560]{1,0:T(8,128)(2,1)} %add_convert_fusion.4) | copy-start | bytes 7864324
  1043.3 16.9 %copy-start.9 = (bf16[512,2048]{1,0:T(8,128)(2,1)S(1)}, bf16[512,2048]{1,0:T(8,128)(2,1)}, u32[]{:S(2)}) copy-start(bf16[512,2048]{1,0:T(8,128)(2,1)} %select_reduce_fusion.1) | copy-start | bytes 6291460
  1060.2 8.4 copy-start.5
  1060.2 8.4 copy-start.19
  1060.2 8.5 copy-start.24
  1085.2 61.5 %copy-start.8 = (bf16[512,2048]{1,0:T(8,128)(2,1)S(1)}, bf16[512,2048]{1,0:T(8,128)(2,1)}, u32[]{:S(2)}) copy-start(bf16[512,2048]{1,0:T(8,128)(2,1)} %convert_element_type.121) | copy-start | bytes 6291460
Sparse Core Ops, SparseCore 0:
  10.2 161.5 all-gather.2
  174.1 257.0 all-gather.4
where the time goes:
time: 1170 us
  matrix products  898 us (77%)
  waiting for transfers between devices  182 us (16%)
  other arithmetic  41 us (4%)
  starting transfers between devices  23.2 us (2%)
  between operations  14.6 us (1%)
    dot_general x37, matrix products, dot_f32(): return lax.dot_general(lhs, rhs, dims, preferred_element_type=jnp.float32)  898 us
    all_to_all x4, waiting for transfers between devices, send_back(): return lax.all_to_all(rows, 'ep', 0, 0, tiled=True)  114 us
    all_gather x1, waiting for transfers between devices, local_body(): x_all = lax.all_gather(x_loc, 'ep', axis=0, tiled=True)  56.5 us
  transfers between devices with their start and end apart: 7, of which 5 were waited for; matrix products, arithmetic and copies ran while one was open for 78% of the time, Pallas kernels for 0%

commit v1 on v0

--- a/solution.py
+++ b/solution.py
@@ -101,6 +101,16 @@
         def send_back(rows):
             return lax.all_to_all(rows, 'ep', 0, 0, tiled=True)
 
+        def swap_back(rows):
+            blocks = rows.reshape(n_dev, -1, d_model)
+            own = lax.dynamic_slice_in_dim(blocks, me, 1, 0)
+            got = lax.dynamic_update_slice_in_dim(jnp.zeros_like(blocks), own, me, 0)
+            for step in range(1, n_dev):
+                block = lax.dynamic_slice_in_dim(blocks, me ^ step, 1, 0)
+                block = lax.ppermute(block, 'ep', [(i, i ^ step) for i in range(n_dev)])
+                got = lax.dynamic_update_slice_in_dim(got, block, me ^ step, 0)
+            return got.reshape(-1, d_model)
+
         def forward(bounds, x_all):
             x_rows = pick(match_of(*bounds).astype(jnp.bfloat16), x_all)
             return x_rows, expert_forward(x_rows, w_gate, w_up, w_down)
@@ -117,6 +127,9 @@
         order = lax.optimization_barrier
         out_back_a, out_b, dy_all, x_all = order((out_back_a, out_b, dy_all, x_all))
         out_back_b = send_back(out_b)
+        q_a, du_a, dv_a, dx_a = backward(chunks[0], dy_all, saved_a)
+        dx_a, dy_all = order((dx_a, dy_all))
+        dx_back_a = swap_back(dx_a)
         q_b, du_b, dv_b, dx_b = backward(chunks[1], dy_all, saved_b)
         dx_b, x_all, dy_all = order((dx_b, x_all, dy_all))
 
@@ -133,25 +146,22 @@
         dguh = dot_f32(x_all, jnp.concatenate([du_p, dv_p], axis=1), CONTRACT_FIRST)
         hot_ddown = dot_f32(hid_p, q_all, CONTRACT_FIRST)
 
-        out_back_b, dx_b, dguh, hot_ddown, dy_all = order((out_back_b, dx_b, dguh, hot_ddown, dy_all))
+        out_back_b, dx_b, dguh, hot_ddown, q_a, q_b, du_a, du_b, dv_a, dv_b = order(
+            (out_back_b, dx_b, dguh, hot_ddown, q_a, q_b, du_a, du_b, dv_a, dv_b))
         dx_back_b = send_back(dx_b)
 
         def both(rows_a, grads_a, rows_b, grads_b):
             return dot_f32(rows_b, grads_b, CONTRACT_FIRST) + dot_f32(rows_a, grads_a, CONTRACT_FIRST)
 
-        q_a, du_a, dv_a, dx_a = backward(chunks[0], dy_all, saved_a)
         grad_down = both(hidden_a, q_a, hidden_b, q_b)
         grad_up = both(x_a, dv_a, x_b, dv_b)
-        dx_back_b, dx_a, grad_down, grad_up, du_a, du_b, out_back_a, out_back_b = order(
-            (dx_back_b, dx_a, grad_down, grad_up, du_a, du_b, out_back_a, out_back_b))
-        dx_back_a = send_back(dx_a)
         grad_gate = both(x_a, du_a, x_b, du_b)
 
         (gate_mix_a, plain_mix_a), (gate_mix_b, plain_mix_b) = mixes
         y_loc = dot_f32(gate_mix_b, out_back_b) + dot_f32(gate_mix_a, out_back_a) + gate_hot[:, None] * out_hot.astype(jnp.float32)
-        dx_part = dot_f32(plain_mix_b, dx_back_b) + dx_hot.astype(jnp.float32)
+        dx_part = dot_f32(plain_mix_a, dx_back_a) + dx_hot.astype(jnp.float32)
         dx_part = lax.optimization_barrier(dx_part)
-        dx_loc = dot_f32(plain_mix_a, dx_back_a) + dx_part
+        dx_loc = dot_f32(plain_mix_b, dx_back_b) + dx_part
         return (y_loc.astype(jnp.bfloat16), dx_loc.astype(jnp.bfloat16), grad_gate[None], grad_up[None], grad_down[None],
                 dguh[:, :part], dguh[:, part:], hot_ddown)
 

time: 1170 us -> 1260 us (1.077)
  waiting for transfers between devices: 182 us -> 221 us
  local copies, waits for them, and re-layouts: 6.77 us -> 40 us
  starting transfers between devices: 23.2 us -> 37.7 us
    ppermute x0 -> x15, waiting for transfers between devices: none -> 103 us  [swap_back(): block = lax.ppermute(block, 'ep', [(i, i ^ step) for i in range(n_dev)])]
    all_to_all x4 -> x3, waiting for transfers between devices: 114 us -> 50.2 us  [send_back(): return lax.all_to_all(rows, 'ep', 0, 0, tiled=True)]
    ppermute x0 -> x15, starting transfers between devices: none -> 19.4 us  [swap_back(): block = lax.ppermute(block, 'ep', [(i, i ^ step) for i in range(n_dev)])]
    dynamic_update_slice x0 -> x15, local copies, waits for them, and re-layouts: none -> 18.6 us  [swap_back(): got = lax.dynamic_update_slice_in_dim(got, block, me ^ step, 0)]
  transfers between devices with their start and end apart: 7 -> 21, of which waited for: 5 -> 12; matrix products, arithmetic and copies ran while one was open for 78% -> 77% of each run, Pallas kernels for 0% -> 0%
where the time goes in v1:
time: 1260 us
  matrix products  897 us (71%)
  waiting for transfers between devices  221 us (18%)
  other arithmetic  45.7 us (4%)
  local copies, waits for them, and re-layouts  40 us (3%)
  starting transfers between devices  37.7 us (3%)
  between operations  14.7 us (1%)
    dot_general x37, matrix products, dot_f32(): return lax.dot_general(lhs, rhs, dims, preferred_element_type=jnp.float32)  897 us
    ppermute x15, waiting for transfers between devices, swap_back(): block = lax.ppermute(block, 'ep', [(i, i ^ step) for i in range(n_dev)])  103 us
    all_gather x1, waiting for transfers between devices, local_body(): x_all = lax.all_gather(x_loc, 'ep', axis=0, tiled=True)  56.3 us
    all_to_all x3, waiting for transfers between devices, send_back(): return lax.all_to_all(rows, 'ep', 0, 0, tiled=True)  50.2 us
  transfers between devices with their start and end apart: 21, of which 12 were waited for; matrix products, arithmetic and copies ran while one was open for 77% of the time, Pallas kernels for 0%

profile of v1, /device:TPU:0, one launch (start us, length us, event | category | flops | bytes accessed | tf_op | source)
XLA Modules:
  0.0 1255.6 jit_solution(2267930405351542187)
XLA Ops:
  22.7 13.0 %fusion = pred[512,4096]{1,0:T(8,128)(4,1)S(1)} fusion(f32[512,6]{0,1:T(8,128)S(1)} %broadcast_add_fusion), kind=kLoop, calls=%fused_computation.3 | loop fusion | flops 23068672 | bytes 2109440 | tf_op jit(solution)/shard_map/reduce_or | solution.py:89
  45.5 11.8 fusion.69
  57.3 5.9 fusion.70
  63.3 6.0 convolution_reduce-precision_fusion
  69.3 6.7 convolution_convert_fusion.6
  75.9 13.2 %select_reduce_fusion = bf16[512,4096]{1,0:T(8,128)(2,1)} fusion(f32[512,6]{0,1:T(8,128)S(1)} %convert_element_type.114, f32[512,6]{0,1:T(8,128)S(1)} %broadcast_add_fusion), kind=kLoop, calls=%fused_computation.1 | loop fusion | flops 35651584 | bytes 4218880 | tf_op jit(solution)/shard_map/reduce_sum | solution.py:88
  89.2 14.4 %fusion.45 = f32[512,2560]{1,0:T(8,128)S(1)} fusion(bf16[2560,1536]{1,0:T(8,128)(2,1)} %param.17, f32[512,1536]{1,0:T(8,128)} %fusion.69, f32[512,1536]{1,0:T(8,128)} %convolution_reduce-precision_fusion, f32[512,1536]{1,0:T(8,128)} %fusion.70), kind=kOutput, calls=%fused_computation.85 | convolution fusion | flops 4034396160 | bytes 22544384 | tf_op jit(solution)/shard_map/dot_general | solution.py:17
  103.6 10.1 add_convert_fusion.4
  115.5 56.3 %all-gather.3.cloned.1.call-done = bf16[8192,2560]{1,0:T(8,128)(2,1)} async-done(((bf16[512,2560]{1,0:T(8,128)(2,1)}), bf16[8192,2560]{1,0:T(8,128)(2,1)}) %all-gather.3.cloned.1.call-update) | async-done | bytes 41943056 | tf_op jit(solution)/shard_map/all_gather | solution.py:56
  171.8 28.7 %convolution_convert_fusion.5 = bf16[16,128,2560]{2,1,0:T(8,128)(2,1)} fusion(bf16[16,512,2560]{2,1,0:T(8,128)(2,1)} %bitcast.119, f32[16,512]{1,0:T(8,128)S(1)} %get-tuple-element.91), kind=kOutput, calls=%fused_computation.32 | convolution fusion | flops 5375000576 | bytes 52461568 | tf_op jit(solution)/shard_map/dot_general | solution.py:17
  200.5 23.1 %fusion.26 = f32[2048,1536]{1,0:T(8,128)} fusion(bf16[2048,2560]{1,0:T(8,128)(2,1)} %bitcast.129, bf16[1,2560,1536]{2,1,0:T(8,128)(2,1)} %param.14), kind=kOutput, calls=%fused_computation.51 | convolution fusion | flops 16106127360 | bytes 30932992 | tf_op jit(solution)/shard_map/dot_general | solution.py:17
  223.7 24.9 %multiply_convert_fusion.8 = (bf16[2048,1536]{1,0:T(8,128)(2,1)}, f32[2048,1536]{1,0:T(8,128)}) fusion(f32[2048,1536]{1,0:T(8,128)} %fusion.26, bf16[2048,2560]{1,0:T(8,128)(2,1)S(1)} %bitcast.130, bf16[1,2560,1536]{2,1,0:T(8,128)(2,1)} %param.15), kind=kOutput, calls=%fused_computation.24 | convolution fusion | flops 16125001728 | bytes 49807360 | tf_op jit(solution)/shard_map/dot_general | solution.py:17
  248.6 23.5 %convolution_convert_fusion.3 = bf16[2048,2560]{1,0:T(8,128)(2,1)} fusion(bf16[2048,1536]{1,0:T(8,128)(2,1)} %get-tuple-element.99, bf16[1,1536,2560]{2,1,0:T(8,128)(2,1)} %param.16), kind=kOutput, calls=%fused_computation.27 | convolution fusion | flops 16111370240 | bytes 24641536 | tf_op jit(solution)/shard_map/dot_general | solution.py:17
  276.2 22.9 %convolution_convert_fusion.2 = bf16[16,256,2560]{2,1,0:T(8,128)(2,1)} fusion(bf16[16,512,2560]{2,1,0:T(8,128)(2,1)} %bitcast.120, f32[16,512]{1,0:T(8,128)S(1)} %get-tuple-element.91, f32[256]{0:T(256)S(1)} %copy-done.20), kind=kOutput, calls=%fused_computation.16 | convolution fusion | flops 10750001152 | bytes 62948352 | tf_op jit(solution)/shard_map/dot_general | solution.py:17
  299.1 40.6 %fusion.24 = f32[4096,1536]{1,0:T(8,128)} fusion(bf16[4096,2560]{1,0:T(8,128)(2,1)} %bitcast.123, bf16[1,2560,1536]{2,1,0:T(8,128)(2,1)} %param.14), kind=kOutput, calls=%fused_computation.49 | convolution fusion | flops 32212254720 | bytes 54001664 | tf_op jit(solution)/shard_map/dot_general | solution.py:17
  339.8 43.8 %multiply_convert_fusion.3 = (bf16[4096,1536]{1,0:T(8,128)(2,1)}, f32[4096,1536]{1,0:T(8,128)}) fusion(f32[4096,1536]{1,0:T(8,128)} %fusion.24, bf16[4096,2560]{1,0:T(8,128)(2,1)} %bitcast.124, bf16[1,2560,1536]{2,1,0:T(8,128)(2,1)} %param.15), kind=kOutput, calls=%fused_computation.7 | convolution fusion | flops 32250003456 | bytes 91750400 | tf_op jit(solution)/shard_map/dot_general | solution.py:17
  383.6 37.3 %convolution_convert_fusion = bf16[4096,2560]{1,0:T(8,128)(2,1)} fusion(bf16[4096,1536]{1,0:T(8,128)(2,1)} %get-tuple-element.101, bf16[1,1536,2560]{2,1,0:T(8,128)(2,1)S(1)} %bitcast.150), kind=kOutput, calls=%fused_computation.13 | convolution fusion | flops 32222740480 | bytes 41418752 | tf_op jit(solution)/shard_map/dot_general | solution.py:17
  420.9 10.3 all-gather.5.cloned.1.call-done
  431.2 17.0 %all-to-all-done.1 = bf16[16,128,2560]{2,1,0:T(8,128)(2,1)} async-done(((bf16[16,128,2560]{2,1,0:T(8,128)(2,1)}), bf16[16,128,2560]{2,1,0:T(8,128)(2,1)}, u32[]{:S(2)}, u32[]{:S(2)}) %all-to-all-start.1) | async-done | bytes 10485792 | tf_op jit(solution)/shard_map/all_to_all | solution.py:102
  452.7 28.6 %convolution_convert_fusion.4 = bf16[16,128,2560]{2,1,0:T(8,128)(2,1)} fusion(bf16[16,512,2560]{2,1,0:T(8,128)(2,1)} %bitcast.117, f32[16,512]{1,0:T(8,128)S(1)} %copy-done.2, bf16[16,512]{1,0:T(8,128)(2,1)S(1)} %copy-done.7), kind=kOutput, calls=%fused_computation.31 | convolution fusion | flops 5376049152 | bytes 52477952 | tf_op jit(solution)/shard_map/dot_general | solution.py:17
  481.4 32.4 %multiply_convert_fusion.6 = (bf16[2048,1536]{1,0:T(8,128)(2,1)}, bf16[2048,1536]{1,0:T(8,128)(2,1)}) fusion(f32[2048,1536]{1,0:T(8,128)} %fusion.26, f32[2048,1536]{1,0:T(8,128)} %get-tuple-element.100, bf16[2048,2560]{1,0:T(8,128)(2,1)} %bitcast.135, bf16[1,1536,2560]{2,1,0:T(8,128)(2,1)} %param.16), kind=kOutput, calls=%fused_computation.22 | convolution fusion | flops 16150167552 | bytes 56098816 | tf_op jit(solution)/shard_map/dot_general | solution.py:17
  513.7 23.1 %fusion.22 = f32[2048,2560]{1,0:T(8,128)} fusion(bf16[2048,1536]{1,0:T(8,128)(2,1)} %get-tuple-element.57, bf16[1,2560,1536]{2,1,0:T(8,128)(2,1)} %param.14), kind=kOutput, calls=%fused_computation.47 | convolution fusion | flops 16106127360 | bytes 35127296 | tf_op jit(solution)/shard_map/dot_general | solution.py:17
  536.8 25.0 %add_convert_fusion.1 = bf16[2048,2560]{1,0:T(8,128)(2,1)} fusion(f32[2048,2560]{1,0:T(8,128)} %fusion.22, bf16[2048,1536]{1,0:T(8,128)(2,1)} %get-tuple-element.59, bf16[1,2560,1536]{2,1,0:T(8,128)(2,1)} %param.15), kind=kOutput, calls=%fused_computation.14 | convolution fusion | flops 16116613120 | bytes 45613056 | tf_op jit(solution)/shard_map/dot_general | solution.py:17
  567.0 8.0 constant_dynamic-slice_fusion
  582.7 22.9 %convolution_convert_fusion.1 = bf16[16,256,2560]{2,1,0:T(8,128)(2,1)} fusion(bf16[16,512,2560]{2,1,0:T(8,128)(2,1)} %bitcast.118, f32[16,512]{1,0:T(8,128)S(1)} %copy-done.2, f32[256]{0:T(256)S(1)} %copy-done.21, bf16[16,512]{1,0:T(8,128)(2,1)S(1)} %copy-done.7), kind=kOutput, calls=%fused_computation.15 | convolution fusion | flops 10752098304 | bytes 62964736 | tf_op jit(solution)/shard_map/dot_general | solution.py:17
  605.6 48.1 %multiply_convert_fusion.1 = (bf16[4096,1536]{1,0:T(8,128)(2,1)}, bf16[4096,1536]{1,0:T(8,128)(2,1)}) fusion(f32[4096,1536]{1,0:T(8,128)} %fusion.24, f32[4096,1536]{1,0:T(8,128)} %get-tuple-element.102, bf16[4096,2560]{1,0:T(8,128)(2,1)} %bitcast.121, bf16[1,1536,2560]{2,1,0:T(8,128)(2,1)} %param.16), kind=kOutput, calls=%fused_computation.5 | convolution fusion | flops 32300335104 | bytes 104333312 | tf_op jit(solution)/shard_map/dot_general | solution.py:17
  653.6 41.5 %fusion.20 = f32[4096,2560]{1,0:T(8,128)} fusion(bf16[4096,1536]{1,0:T(8,128)(2,1)} %get-tuple-element.56, bf16[1,2560,1536]{2,1,0:T(8,128)(2,1)} %param.14), kind=kOutput, calls=%fused_computation.45 | convolution fusion | flops 32212254720 | bytes 62390272 | tf_op jit(solution)/shard_map/dot_general | solution.py:17
  695.1 43.6 %add_convert_fusion = bf16[4096,2560]{1,0:T(8,128)(2,1)} fusion(f32[4096,2560]{1,0:T(8,128)} %fusion.20, bf16[4096,1536]{1,0:T(8,128)(2,1)} %get-tuple-element.58, bf16[1,2560,1536]{2,1,0:T(8,128)(2,1)} %param.15), kind=kOutput, calls=%fused_computation.4 | convolution fusion | flops 32233226240 | bytes 83361792 | tf_op jit(solution)/shard_map/dot_general | solution.py:17
  738.7 22.4 %fusion.47 = f32[8192,192]{0,1:T(8,128)} fusion(bf16[8192,2560]{1,0:T(8,128)(2,1)} %all-gather.3.cloned.1.call-done, bf16[2560,96]{1,0:T(8,128)(2,1)S(1)} %copy-done.18, bf16[2560,96]{1,0:T(8,128)(2,1)S(1)} %copy-done.19), kind=kOutput, calls=%fused_computation.87 | convolution fusion | flops 8055029760 | bytes 49217536 | tf_op jit(solution)/shard_map/dot_general | solution.py:17
  761.1 22.3 %multiply_convert_fusion.14 = (bf16[8192,96]{0,1:T(8,128)(2,1)S(1)}, bf16[8192,96]{0,1:T(8,128)(2,1)}) fusion(f32[8192,192]{0,1:T(8,128)} %fusion.47, bf16[1536,2560]{1,0:T(8,128)(2,1)} %param.19, s32[]{:T(128)S(6)} %select_n.108, bf16[8192,2560]{1,0:T(8,128)(2,1)} %all-gather.5.cloned.1.call-done, f32[8192]{0:T(1024)S(1)} %bitcast.144), kind=kOutput, calls=%fused_computation.72 | convolution fusion | flops 4100456448 | bytes 51904516 | tf_op jit(solution)/shard_map/dot_general | solution.py:17
  783.4 19.0 %fusion.33 = f32[2560,192]{0,1:T(8,128)} fusion(bf16[8192,2560]{1,0:T(8,128)(2,1)} %all-gather.3.cloned.1.call-done, bf16[8192,96]{0,1:T(8,128)(2,1)} %get-tuple-element.87, bf16[8192,96]{0,1:T(8,128)(2,1)S(1)} %get-tuple-element.86), kind=kOutput, calls=%fused_computation.66 | convolution fusion | flops 8059355136 | bytes 47054848 | tf_op jit(solution)/shard_map/dot_general | solution.py:17
  802.4 20.2 %fusion.3 = f32[96,2560]{1,0:T(8,128)} fusion(bf16[8192,2560]{1,0:T(8,128)(2,1)} %all-gather.5.cloned.1.call-done, f32[8192]{0:T(1024)S(1)} %bitcast.145, f32[8192,192]{0,1:T(8,128)} %fusion.47), kind=kOutput, calls=%fused_computation.17 | convolution fusion | flops 4094164992 | bytes 49250304 | tf_op jit(solution)/shard_map/dot_general | solution.py:17
  822.6 10.0 fusion.71
  837.7 11.5 collective-permute-done.2
  855.0 24.5 %collective-permute-done.4 = bf16[1,128,2560]{2,1,0:T(8,128)(2,1)S(1)} collective-permute-done((bf16[1,128,2560]{2,1,0:T(8,128)(2,1)S(1)}, bf16[1,128,2560]{2,1,0:T(8,128)(2,1)S(1)}, u32[]{:S(2)}, u32[]{:S(2)}) %collective-permute-start.4) | collective-permute-done | bytes 655392 | tf_op jit(solution)/shard_map/ppermute | solution.py:110
  883.2 13.4 %collective-permute-done.6 = bf16[1,128,2560]{2,1,0:T(8,128)(2,1)S(1)} collective-permute-done((bf16[1,128,2560]{2,1,0:T(8,128)(2,1)S(1)}, bf16[1,128,2560]{2,1,0:T(8,128)(2,1)S(1)}, u32[]{:S(2)}, u32[]{:S(2)}) %collective-permute-start.6) | collective-permute-done | bytes 655392 | tf_op jit(solution)/shard_map/ppermute | solution.py:110
  901.3 25.5 %collective-permute-done.8 = bf16[1,128,2560]{2,1,0:T(8,128)(2,1)S(1)} collective-permute-done((bf16[1,128,2560]{2,1,0:T(8,128)(2,1)S(1)}, bf16[1,128,2560]{2,1,0:T(8,128)(2,1)S(1)}, u32[]{:S(2)}, u32[]{:S(2)}) %collective-permute-start.8) | collective-permute-done | bytes 655392 | tf_op jit(solution)/shard_map/ppermute | solution.py:110
  931.7 23.5 %collective-permute-done.10 = bf16[1,128,2560]{2,1,0:T(8,128)(2,1)S(1)} collective-permute-done((bf16[1,128,2560]{2,1,0:T(8,128)(2,1)S(1)}, bf16[1,128,2560]{2,1,0:T(8,128)(2,1)S(1)}, u32[]{:S(2)}, u32[]{:S(2)}) %collective-permute-start.10) | collective-permute-done | bytes 655392 | tf_op jit(solution)/shard_map/ppermute | solution.py:110
  965.6 9.8 convert_add_fusion
  982.7 41.4 %fusion.75 = f32[1536,2560]{1,0:T(8,128)} fusion(bf16[4096,1536]{1,0:T(8,128)(2,1)} %get-tuple-element.101, bf16[4096,2560]{1,0:T(8,128)(2,1)} %bitcast.122), kind=kOutput, calls=%fused_computation.165 | convolution fusion | flops 32212254720 | bytes 49283072 | tf_op jit(solution)/shard_map/dot_general | solution.py:17
  1024.2 21.1 %fusion.73 = f32[2560,1536]{1,0:T(8,128)} fusion(bf16[2048,2560]{1,0:T(8,128)(2,1)S(1)} %bitcast.133, bf16[2048,1536]{1,0:T(8,128)(2,1)} %get-tuple-element.57), kind=kOutput, calls=%fused_computation.163 | convolution fusion | flops 16106127360 | bytes 32505856 | tf_op jit(solution)/shard_map/dot_general | solution.py:17
  1045.3 18.6 %add_convert_fusion.3 = bf16[512,2560]{1,0:T(8,128)(2,1)} fusion(bf16[512,2560]{1,0:T(8,128)(2,1)S(1)} %copy-done.30, f32[512,2560]{1,0:T(8,128)} %fusion.71, bf16[512,4096]{1,0:T(8,128)(2,1)} %select_reduce_fusion, bf16[4096,2560]{1,0:T(8,128)(2,1)} %bitcast.14, f32[512]{0:T(512)S(1)} %bitcast.148), kind=kOutput, calls=%fused_computation.55 | convolution fusion | flops 10743971840 | bytes 35653632 | tf_op jit(solution)/shard_map/dot_general | solution.py:17
  1063.9 25.5 %add_bitcast_fusion = f32[1,1536,2560]{2,1,0:T(8,128)} fusion(f32[1536,2560]{1,0:T(8,128)} %fusion.75, bf16[2048,1536]{1,0:T(8,128)(2,1)} %get-tuple-element.99, bf16[2048,2560]{1,0:T(8,128)(2,1)} %bitcast.136), kind=kOutput, calls=%fused_computation.19 | convolution fusion | flops 16110059520 | bytes 48234496 | tf_op jit(solution)/shard_map/dot_general | solution.py:17
  1089.3 21.4 %fusion.74 = f32[2560,1536]{1,0:T(8,128)} fusion(bf16[2048,2560]{1,0:T(8,128)(2,1)S(1)} %bitcast.134, bf16[2048,1536]{1,0:T(8,128)(2,1)} %get-tuple-element.59), kind=kOutput, calls=%fused_computation.164 | convolution fusion | flops 16106127360 | bytes 32505856 | tf_op jit(solution)/shard_map/dot_general | solution.py:17
  1110.7 42.3 %add_bitcast_fusion.2 = f32[1,2560,1536]{2,1,0:T(8,128)} fusion(f32[2560,1536]{1,0:T(8,128)} %fusion.73, bf16[4096,2560]{1,0:T(8,128)(2,1)} %bitcast.125, bf16[4096,1536]{1,0:T(8,128)(2,1)} %get-tuple-element.56), kind=kOutput, calls=%fused_computation.21 | convolution fusion | flops 32216186880 | bytes 65011712 | tf_op jit(solution)/shard_map/dot_general | solution.py:17
  1153.0 42.4 %add_bitcast_fusion.1 = f32[1,2560,1536]{2,1,0:T(8,128)} fusion(f32[2560,1536]{1,0:T(8,128)S(1)} %copy-done.29, bf16[4096,2560]{1,0:T(8,128)(2,1)} %bitcast.126, bf16[4096,1536]{1,0:T(8,128)(2,1)} %get-tuple-element.58), kind=kOutput, calls=%fused_computation.20 | convolution fusion | flops 32216186880 | bytes 65011712 | tf_op jit(solution)/shard_map/dot_general | solution.py:17
  1195.4 33.2 %all-to-all-done.3 = bf16[16,256,2560]{2,1,0:T(8,128)(2,1)} async-done(((bf16[16,256,2560]{2,1,0:T(8,128)(2,1)}), bf16[16,256,2560]{2,1,0:T(8,128)(2,1)}, u32[]{:S(2)}, u32[]{:S(2)}) %all-to-all-start.3) | async-done | bytes 20971552 | tf_op jit(solution)/shard_map/all_to_all | solution.py:102
  1228.6 15.2 %fusion.72 = f32[512,2560]{1,0:T(8,128)S(1)} fusion(bf16[512,4096]{1,0:T(8,128)(2,1)} %convert_element_type.123, bf16[4096,2560]{1,0:T(8,128)(2,1)} %bitcast.20), kind=kOutput, calls=%fused_computation.162 | convolution fusion | flops 10737418240 | bytes 30408704 | tf_op jit(solution)/shard_map/dot_general | solution.py:17
  (162 shorter events, 95.2 us)
Async XLA Ops:
  7.2 164.7 %all-gather.3.cloned.1.call-start = ((), (), s32[]{:S(2)}) async-start(), calls=%async_computation.4 | async-start | bytes 44564480 | tf_op jit(solution)/shard_map/all_gather | solution.py:56
  7.9 423.3 %all-gather.5.cloned.1.call-start = ((), (), s32[]{:S(2)}) async-start(), calls=%async_computation.5 | async-start | bytes 44564480 | tf_op jit(solution)/shard_map/all_gather | solution.py:57
  10.1 53.1 %copy-start.23 = (f32[512,1]{0,1:T(1,128)}, f32[512,1]{0,1:T(1,128)S(1)}, u32[]{:S(2)}) copy-start(f32[512,1]{0,1:T(1,128)S(1)} %slice.54) | copy-start | bytes 6148
  12.0 102.2 %all-to-all-start = ((f32[16,1,1536]{2,1,0:T(1,128)}), f32[16,1,1536]{2,1,0:T(1,128)S(1)}, u32[]{:S(2)}, u32[]{:S(2)}) async-start(f32[16,1,1536]{2,1,0:T(1,128)} %copy.37), calls=%async_computation | async-start | bytes 196608 | tf_op jit(solution)/shard_map/all_to_all | solution.py:70
  45.5 17.7 %slice-start.7 = ((s8[7864320]{0:T(1024)(128)(4,1)}), s8[4194304]{0:T(1024)(128)(4,1)S(1)}, s32[]{:S(2)}) async-start(s8[7864320]{0:T(1024)(128)(4,1)} %bitcast.151), calls=%async_computation.13 | async-start | bytes 8388608
  114.9 161.3 %copy-start.1 = (f32[16,512]{1,0:T(8,128)}, f32[16,512]{1,0:T(8,128)S(1)}, u32[]{:S(2)}) copy-start(f32[16,512]{1,0:T(8,128)S(1)} %get-tuple-element.91) | copy-start | bytes 98308
  200.5 23.1 %copy-start = (bf16[16,128,2560]{2,1,0:T(8,128)(2,1)S(1)}, bf16[16,128,2560]{2,1,0:T(8,128)(2,1)}, u32[]{:S(2)}) copy-start(bf16[16,128,2560]{2,1,0:T(8,128)(2,1)} %convolution_convert_fusion.5) | copy-start | bytes 31457284
  272.1 176.1 %all-to-all-start.1 = ((bf16[16,128,2560]{2,1,0:T(8,128)(2,1)}), bf16[16,128,2560]{2,1,0:T(8,128)(2,1)}, u32[]{:S(2)}, u32[]{:S(2)}) async-start(bf16[16,128,2560]{2,1,0:T(8,128)(2,1)} %bitcast.138), calls=%async_computation.1 | async-start | bytes 20971520 | tf_op jit(solution)/shard_map/all_to_all | solution.py:102
  299.1 84.5 %slice-start.5 = ((s8[7864320]{0:T(1024)(128)(4,1)}), s8[4194304]{0:T(1024)(128)(4,1)S(1)}, s32[]{:S(2)}) async-start(s8[7864320]{0:T(1024)(128)(4,1)} %bitcast.149), calls=%async_computation.11 | async-start | bytes 8388608
  339.8 43.8 %slice-start.6 = ((s8[7864320]{0:T(1024)(128)(4,1)}), s8[3670016]{0:T(1024)(128)(4,1)S(1)}, s32[]{:S(2)}) async-start(s8[7864320]{0:T(1024)(128)(4,1)} %bitcast.149), calls=%async_computation.12 | async-start | bytes 7340032
  448.2 527.2 %all-to-all-start.2 = ((bf16[16,256,2560]{2,1,0:T(8,128)(2,1)}), bf16[16,256,2560]{2,1,0:T(8,128)(2,1)}, u32[]{:S(2)}, u32[]{:S(2)}) async-start(bf16[16,256,2560]{2,1,0:T(8,128)(2,1)} %bitcast.127), calls=%async_computation.2 | async-start | bytes 41943040 | tf_op jit(solution)/shard_map/all_to_all | solution.py:102
  567.0 15.7 %copy-start.21 = (f32[256]{0:T(256)S(1)}, f32[256]{0:T(256)}, u32[]{:S(2)}) copy-start(f32[256]{0:T(256)} %iota_add_fusion) | copy-start | bytes 3076
  574.9 388.7 %collective-permute-start.14 = (bf16[1,128,2560]{2,1,0:T(8,128)(2,1)}, bf16[1,128,2560]{2,1,0:T(8,128)(2,1)}, u32[]{:S(2)}, u32[]{:S(2)}) collective-permute-start(bf16[1,128,2560]{2,1,0:T(8,128)(2,1)} %get-tuple-element.70), channel_id=1, source_target_pairs={{0,15},{1,14},{2,13},{3,12},{4,11},{5,10},{6,9},{7,8},{8,7},{9,6},... | collective-permute-start | bytes 1966088 | tf_op jit(solution)/shard_map/ppermute | solution.py:110
  578.4 383.2 %collective-permute-start.13 = (bf16[1,128,2560]{2,1,0:T(8,128)(2,1)}, bf16[1,128,2560]{2,1,0:T(8,128)(2,1)}, u32[]{:S(2)}, u32[]{:S(2)}) collective-permute-start(bf16[1,128,2560]{2,1,0:T(8,128)(2,1)} %get-tuple-element.71), channel_id=1, source_target_pairs={{0,14},{1,15},{2,12},{3,13},{4,10},{5,11},{6,8},{7,9},{8,6},{9,7},... | collective-permute-start | bytes 1966088 | tf_op jit(solution)/shard_map/ppermute | solution.py:110
  578.7 380.9 %collective-permute-start.12 = (bf16[1,128,2560]{2,1,0:T(8,128)(2,1)}, bf16[1,128,2560]{2,1,0:T(8,128)(2,1)}, u32[]{:S(2)}, u32[]{:S(2)}) collective-permute-start(bf16[1,128,2560]{2,1,0:T(8,128)(2,1)} %get-tuple-element.72), channel_id=1, source_target_pairs={{0,13},{1,12},{2,15},{3,14},{4,9},{5,8},{6,11},{7,10},{8,5},{9,4},... | collective-permute-start | bytes 1966088 | tf_op jit(solution)/shard_map/ppermute | solution.py:110
  581.1 254.1 %collective-permute-start.1 = (bf16[1,128,2560]{2,1,0:T(8,128)(2,1)}, bf16[1,128,2560]{2,1,0:T(8,128)(2,1)}, u32[]{:S(2)}, u32[]{:S(2)}) collective-permute-start(bf16[1,128,2560]{2,1,0:T(8,128)(2,1)} %get-tuple-element.83), channel_id=1, source_target_pairs={{0,2},{1,3},{2,0},{3,1},{4,6},{5,7},{6,4},{7,5},{8,10},{9,11},{10,... | collective-permute-start | bytes 1966088 | tf_op jit(solution)/shard_map/ppermute | solution.py:110
  582.5 250.1 %collective-permute-start = (bf16[1,128,2560]{2,1,0:T(8,128)(2,1)}, bf16[1,128,2560]{2,1,0:T(8,128)(2,1)}, u32[]{:S(2)}, u32[]{:S(2)}) collective-permute-start(bf16[1,128,2560]{2,1,0:T(8,128)(2,1)} %get-tuple-element.84), channel_id=1, source_target_pairs={{0,1},{1,0},{2,3},{3,2},{4,5},{5,4},{6,7},{7,6},{8,9},{9,8},{10,11... | collective-permute-start | bytes 1966088 | tf_op jit(solution)/shard_map/ppermute | solution.py:110
  695.1 43.6 %copy-start.18 = (bf16[2560,96]{1,0:T(8,128)(2,1)S(1)}, bf16[2560,96]{1,0:T(8,128)(2,1)}, u32[]{:S(2)}) copy-start(bf16[2560,96]{1,0:T(8,128)(2,1)} %get-tuple-element.105) | copy-start | bytes 1474564
  695.1 43.6 %copy-start.19 = (bf16[2560,96]{1,0:T(8,128)(2,1)S(1)}, bf16[2560,96]{1,0:T(8,128)(2,1)}, u32[]{:S(2)}) copy-start(bf16[2560,96]{1,0:T(8,128)(2,1)} %get-tuple-element.106) | copy-start | bytes 1474564
  738.7 22.4 %copy-start.22 = (f32[2,4,8,128]{3,1,2,0:T(4,128)S(1)}, f32[2,4,8,128]{3,1,2,0:T(4,128)}, u32[]{:S(2)}) copy-start(f32[2,4,8,128]{3,1,2,0:T(4,128)} %copy.43) | copy-start | bytes 98308
  802.3 20.2 %copy-start.6 = (bf16[512,2048]{1,0:T(8,128)(2,1)S(1)}, bf16[512,2048]{1,0:T(8,128)(2,1)}, u32[]{:S(2)}) copy-start(bf16[512,2048]{1,0:T(8,128)(2,1)} %select_reduce_fusion.1) | copy-start | bytes 6291460
  822.6 26.6 %copy-start.15 = (bf16[1,128,2560]{2,1,0:T(8,128)(2,1)S(1)}, bf16[1,128,2560]{2,1,0:T(8,128)(2,1)}, u32[]{:S(2)}) copy-start(bf16[1,128,2560]{2,1,0:T(8,128)(2,1)} %get-tuple-element.80) | copy-start | bytes 1966084
  822.6 29.5 %copy-start.14 = (bf16[1,128,2560]{2,1,0:T(8,128)(2,1)S(1)}, bf16[1,128,2560]{2,1,0:T(8,128)(2,1)}, u32[]{:S(2)}) copy-start(bf16[1,128,2560]{2,1,0:T(8,128)(2,1)} %get-tuple-element.79) | copy-start | bytes 1966084
  822.6 56.8 %copy-start.13 = (bf16[1,128,2560]{2,1,0:T(8,128)(2,1)S(1)}, bf16[1,128,2560]{2,1,0:T(8,128)(2,1)}, u32[]{:S(2)}) copy-start(bf16[1,128,2560]{2,1,0:T(8,128)(2,1)} %get-tuple-element.78) | copy-start | bytes 1966084
  822.6 59.2 %copy-start.12 = (bf16[1,128,2560]{2,1,0:T(8,128)(2,1)S(1)}, bf16[1,128,2560]{2,1,0:T(8,128)(2,1)}, u32[]{:S(2)}) copy-start(bf16[1,128,2560]{2,1,0:T(8,128)(2,1)} %get-tuple-element.77) | copy-start | bytes 1966084
  822.6 73.9 %copy-start.11 = (bf16[1,128,2560]{2,1,0:T(8,128)(2,1)S(1)}, bf16[1,128,2560]{2,1,0:T(8,128)(2,1)}, u32[]{:S(2)}) copy-start(bf16[1,128,2560]{2,1,0:T(8,128)(2,1)} %get-tuple-element.76) | copy-start | bytes 1966084
  832.6 65.8 %copy-start.10 = (bf16[1,128,2560]{2,1,0:T(8,128)(2,1)S(1)}, bf16[1,128,2560]{2,1,0:T(8,128)(2,1)}, u32[]{:S(2)}) copy-start(bf16[1,128,2560]{2,1,0:T(8,128)(2,1)} %get-tuple-element.75) | copy-start | bytes 1966084
  832.6 94.2 %copy-start.9 = (bf16[1,128,2560]{2,1,0:T(8,128)(2,1)S(1)}, bf16[1,128,2560]{2,1,0:T(8,128)(2,1)}, u32[]{:S(2)}) copy-start(bf16[1,128,2560]{2,1,0:T(8,128)(2,1)} %get-tuple-element.74) | copy-start | bytes 1966084
  832.6 96.6 %copy-start.8 = (bf16[1,128,2560]{2,1,0:T(8,128)(2,1)S(1)}, bf16[1,128,2560]{2,1,0:T(8,128)(2,1)}, u32[]{:S(2)}) copy-start(bf16[1,128,2560]{2,1,0:T(8,128)(2,1)} %get-tuple-element.73) | copy-start | bytes 1966084
  832.6 16.5 %collective-permute-start.2 = (bf16[1,128,2560]{2,1,0:T(8,128)(2,1)S(1)}, bf16[1,128,2560]{2,1,0:T(8,128)(2,1)S(1)}, u32[]{:S(2)}, u32[]{:S(2)}) collective-permute-start(bf16[1,128,2560]{2,1,0:T(8,128)(2,1)S(1)} %copy-done.17), channel_id=1, source_target_pairs={{0,3},{1,2},{2,1},{3,0},{4,7},{5,6},{6,5},{7,4},{8,11},{9,10},{10,... | collective-permute-start | bytes 1966088 | tf_op jit(solution)/shard_map/ppermute | solution.py:110
  835.2 16.9 %collective-permute-start.3 = (bf16[1,128,2560]{2,1,0:T(8,128)(2,1)S(1)}, bf16[1,128,2560]{2,1,0:T(8,128)(2,1)S(1)}, u32[]{:S(2)}, u32[]{:S(2)}) collective-permute-start(bf16[1,128,2560]{2,1,0:T(8,128)(2,1)S(1)} %copy-done.16), channel_id=1, source_target_pairs={{0,4},{1,5},{2,6},{3,7},{4,0},{5,1},{6,2},{7,3},{8,12},{9,13},{10,... | collective-permute-start | bytes 1966088 | tf_op jit(solution)/shard_map/ppermute | solution.py:110
  849.2 116.4 %copy-start.5 = (bf16[512,2048]{1,0:T(8,128)(2,1)S(1)}, bf16[512,2048]{1,0:T(8,128)(2,1)}, u32[]{:S(2)}) copy-start(bf16[512,2048]{1,0:T(8,128)(2,1)} %convert_element_type.121) | copy-start | bytes 6291460
  849.2 116.4 %copy-start.28 = (bf16[512,2560]{1,0:T(8,128)(2,1)S(1)}, bf16[512,2560]{1,0:T(8,128)(2,1)}, u32[]{:S(2)}) copy-start(bf16[512,2560]{1,0:T(8,128)(2,1)} %add_convert_fusion.4) | copy-start | bytes 7864324
  849.2 30.3 %collective-permute-start.4 = (bf16[1,128,2560]{2,1,0:T(8,128)(2,1)S(1)}, bf16[1,128,2560]{2,1,0:T(8,128)(2,1)S(1)}, u32[]{:S(2)}, u32[]{:S(2)}) collective-permute-start(bf16[1,128,2560]{2,1,0:T(8,128)(2,1)S(1)} %copy-done.15), channel_id=1, source_target_pairs={{0,5},{1,4},{2,7},{3,6},{4,1},{5,0},{6,3},{7,2},{8,13},{9,12},{10,... | collective-permute-start | bytes 1966088 | tf_op jit(solution)/shard_map/ppermute | solution.py:110
  852.1 29.7 %collective-permute-start.5 = (bf16[1,128,2560]{2,1,0:T(8,128)(2,1)S(1)}, bf16[1,128,2560]{2,1,0:T(8,128)(2,1)S(1)}, u32[]{:S(2)}, u32[]{:S(2)}) collective-permute-start(bf16[1,128,2560]{2,1,0:T(8,128)(2,1)S(1)} %copy-done.14), channel_id=1, source_target_pairs={{0,6},{1,7},{2,4},{3,5},{4,2},{5,3},{6,0},{7,1},{8,14},{9,15},{10,... | collective-permute-start | bytes 1966088 | tf_op jit(solution)/shard_map/ppermute | solution.py:110
  879.4 17.1 %collective-permute-start.6 = (bf16[1,128,2560]{2,1,0:T(8,128)(2,1)S(1)}, bf16[1,128,2560]{2,1,0:T(8,128)(2,1)S(1)}, u32[]{:S(2)}, u32[]{:S(2)}) collective-permute-start(bf16[1,128,2560]{2,1,0:T(8,128)(2,1)S(1)} %copy-done.13), channel_id=1, source_target_pairs={{0,7},{1,6},{2,5},{3,4},{4,3},{5,2},{6,1},{7,0},{8,15},{9,14},{10,... | collective-permute-start | bytes 1966088 | tf_op jit(solution)/shard_map/ppermute | solution.py:110
  881.8 16.6 %collective-permute-start.7 = (bf16[1,128,2560]{2,1,0:T(8,128)(2,1)S(1)}, bf16[1,128,2560]{2,1,0:T(8,128)(2,1)S(1)}, u32[]{:S(2)}, u32[]{:S(2)}) collective-permute-start(bf16[1,128,2560]{2,1,0:T(8,128)(2,1)S(1)} %copy-done.12), channel_id=1, source_target_pairs={{0,8},{1,9},{2,10},{3,11},{4,12},{5,13},{6,14},{7,15},{8,0},{9,1},... | collective-permute-start | bytes 1966088 | tf_op jit(solution)/shard_map/ppermute | solution.py:110
  896.6 30.2 %collective-permute-start.8 = (bf16[1,128,2560]{2,1,0:T(8,128)(2,1)S(1)}, bf16[1,128,2560]{2,1,0:T(8,128)(2,1)S(1)}, u32[]{:S(2)}, u32[]{:S(2)}) collective-permute-start(bf16[1,128,2560]{2,1,0:T(8,128)(2,1)S(1)} %copy-done.11), channel_id=1, source_target_pairs={{0,9},{1,8},{2,11},{3,10},{4,13},{5,12},{6,15},{7,14},{8,1},{9,0},... | collective-permute-start | bytes 1966088 | tf_op jit(solution)/shard_map/ppermute | solution.py:110
  898.4 30.8 %collective-permute-start.9 = (bf16[1,128,2560]{2,1,0:T(8,128)(2,1)S(1)}, bf16[1,128,2560]{2,1,0:T(8,128)(2,1)S(1)}, u32[]{:S(2)}, u32[]{:S(2)}) collective-permute-start(bf16[1,128,2560]{2,1,0:T(8,128)(2,1)S(1)} %copy-done.10), channel_id=1, source_target_pairs={{0,10},{1,11},{2,8},{3,9},{4,14},{5,15},{6,12},{7,13},{8,2},{9,3},... | collective-permute-start | bytes 1966088 | tf_op jit(solution)/shard_map/ppermute | solution.py:110
  926.8 28.4 %collective-permute-start.10 = (bf16[1,128,2560]{2,1,0:T(8,128)(2,1)S(1)}, bf16[1,128,2560]{2,1,0:T(8,128)(2,1)S(1)}, u32[]{:S(2)}, u32[]{:S(2)}) collective-permute-start(bf16[1,128,2560]{2,1,0:T(8,128)(2,1)S(1)} %copy-done.9), channel_id=1, source_target_pairs={{0,11},{1,10},{2,9},{3,8},{4,15},{5,14},{6,13},{7,12},{8,3},{9,2},... | collective-permute-start | bytes 1966088 | tf_op jit(solution)/shard_map/ppermute | solution.py:110
  929.2 29.6 %collective-permute-start.11 = (bf16[1,128,2560]{2,1,0:T(8,128)(2,1)S(1)}, bf16[1,128,2560]{2,1,0:T(8,128)(2,1)S(1)}, u32[]{:S(2)}, u32[]{:S(2)}) collective-permute-start(bf16[1,128,2560]{2,1,0:T(8,128)(2,1)S(1)} %copy-done.8), channel_id=1, source_target_pairs={{0,12},{1,13},{2,14},{3,15},{4,8},{5,9},{6,10},{7,11},{8,4},{9,5},... | collective-permute-start | bytes 1966088 | tf_op jit(solution)/shard_map/ppermute | solution.py:110
  975.4 48.8 %slice-start = ((s8[10485760]{0:T(1024)(128)(4,1)}), s8[2097152]{0:T(1024)(128)(4,1)S(1)}, s32[]{:S(2)}) async-start(s8[10485760]{0:T(1024)(128)(4,1)} %bitcast.131), calls=%async_computation.6 | async-start | bytes 4194304
  975.4 253.2 %all-to-all-start.3 = ((bf16[16,256,2560]{2,1,0:T(8,128)(2,1)}), bf16[16,256,2560]{2,1,0:T(8,128)(2,1)}, u32[]{:S(2)}, u32[]{:S(2)}) async-start(bf16[16,256,2560]{2,1,0:T(8,128)(2,1)} %bitcast.128), calls=%async_computation.3 | async-start | bytes 41943040 | tf_op jit(solution)/shard_map/all_to_all | solution.py:102
  982.7 41.4 %slice-start.1 = ((s8[10485760]{0:T(1024)(128)(4,1)}), s8[4194304]{0:T(1024)(128)(4,1)S(1)}, s32[]{:S(2)}) async-start(s8[10485760]{0:T(1024)(128)(4,1)} %bitcast.131), calls=%async_computation.7 | async-start | bytes 8388608
  982.7 41.4 %slice-start.2 = ((s8[10485760]{0:T(1024)(128)(4,1)}), s8[4194304]{0:T(1024)(128)(4,1)S(1)}, s32[]{:S(2)}) async-start(s8[10485760]{0:T(1024)(128)(4,1)} %bitcast.131), calls=%async_computation.8 | async-start | bytes 8388608
  1024.2 21.1 %copy-start.24 = (f32[512,1]{0,1:T(1,128)S(1)}, f32[512,1]{0,1:T(1,128)}, u32[]{:S(2)}) copy-start(f32[512,1]{0,1:T(1,128)} %copy-done.23) | copy-start | bytes 6148
  1024.2 21.1 %copy-start.30 = (bf16[512,2560]{1,0:T(8,128)(2,1)S(1)}, bf16[512,2560]{1,0:T(8,128)(2,1)}, u32[]{:S(2)}) copy-start(bf16[512,2560]{1,0:T(8,128)(2,1)} %convolution_convert_fusion.6) | copy-start | bytes 7864324
  1110.7 42.3 %copy-start.29 = (f32[2560,1536]{1,0:T(8,128)S(1)}, f32[2560,1536]{1,0:T(8,128)}, u32[]{:S(2)}) copy-start(f32[2560,1536]{1,0:T(8,128)} %fusion.74) | copy-start | bytes 47185924
  (13 other events, 113.1 us)
Sparse Core Ops, SparseCore 0:
  10.2 161.5 all-gather.2
  174.1 257.0 all-gather.4
